TPU v7x, 128 devices: a whole 4x4x4 slice. The times are simulated.
128 devices in a mesh: side: 2 (over y_lo), gx: 8 (over x, core), gy: 8 (over z, y_hi).
Axes of the slice: x: 4, y: 4 (y_hi: 2, y_lo: 2; y = y_hi * 2 + y_lo), z: 4, core: 2. Of those that a mesh axis runs over, the one named last changes fastest.
Arguments:
- populations: float32 [2, 19, 4, 256, 1024], P('side', None, None, 'gx', 'gy'), may hold values from 0.01 to 0.84, as said below
- solid_mask: int32 [2, 4, 256, 1024], P('side', None, 'gx', 'gy'), may hold values 0 or 1
- water_sheet: float32 [32, 256, 1024], P(None, 'gx', ('side', 'gy')), may hold values from 2 to 12
- current: float32 [256, 1024], P('gx', ('side', 'gy')), may hold values from 0.5 to 3
Outputs:
- populations_out: float32 [2, 19, 4, 256, 1024], P('side', None, None, 'gx', 'gy')
- sheet_out: float32 [32, 256, 1024], P(None, 'gx', ('side', 'gy'))
Inputs may be any that keep to these rules, and one draw needn't show every extreme that they name: `populations`: every population is positive.
All inputs are finite; a program needn't handle non-finite values. No bound on the sum of `solid_mask` on one device may be relied on, other than what follows from the above.
Results may differ from a plain program's by a relative error of at most 0.0003.
Values sent between devices are 32-bit elements; how exact they have to be, the bound alone decides.
A program may use at most 64 MiB of HBM per device.

v0:
```python
import functools

import jax
import jax.numpy as jnp
from jax import lax
from jax.experimental import pallas as pl
from jax.experimental.pallas import tpu as pltpu
from jax.sharding import PartitionSpec as P

STEPS = 8
SUBSTEPS = 2
LATTICE = 19
MESH = pl.DeviceIdType.MESH

velocity_table = (
    (0, 0, 0),
    (1, 0, 0),
    (-1, 0, 0),
    (0, 1, 0),
    (0, -1, 0),
    (0, 0, 1),
    (0, 0, -1),
    (1, 1, 0),
    (-1, -1, 0),
    (1, -1, 0),
    (-1, 1, 0),
    (1, 0, 1),
    (-1, 0, -1),
    (1, 0, -1),
    (-1, 0, 1),
    (0, 1, 1),
    (0, -1, -1),
    (0, 1, -1),
    (0, -1, 1),
)
opposite_index = (0, 2, 1, 4, 3, 6, 5, 8, 7, 10, 9, 12, 11, 14, 13, 16, 15, 18, 17)
weight_table = (1.0 / 3.0,) + (1.0 / 18.0,) * 6 + (1.0 / 36.0,) * 12
relax_time = 0.8
coupling = -3.0
wall_potential = 0.4
uptake_rate = 0.02
drag_rate = 0.03
base_diffusion = 0.05
slope_diffusion = 0.015

PAIRS = 10
PAD = 8
ROWS = 16 * PAIRS + 2 * PAD
MASK_PLANE = LATTICE
FLUX_PLANE = LATTICE + 1
PLANES = LATTICE + 2
RATE = 1.0 / relax_time
KAPPA = RATE / 36.0


def roll(values, shift):
    shift = shift % 128
    if shift == 0:
        return values
    return pltpu.roll(values, shift, values.ndim - 1)


def lanes_of(shape):
    return lax.broadcasted_iota(jnp.int32, shape, len(shape) - 1)


def uptake(density_row):
    activity = density_row / (1.0 + density_row)
    return 0.043 + activity * (17.18 + activity * (-39.85 + 36.0 * activity))


def pack_columns(ref, offset, rows):
    lanes = lanes_of((rows, 128))
    packed = None
    for m in range(4):
        part = roll(ref[pl.ds(m, rows, stride=4), :], 32 * m - offset)
        packed = part if packed is None else jnp.where(lanes >= 32 * m, part, packed)
    return packed


def unpack_columns(packed, ref):
    for m in range(4):
        ref[pl.ds(m, packed.shape[0], stride=4), :] = roll(packed, -32 * m)


def pack_pair(a, b):
    lower = lanes_of(a.shape) % 32 < 16
    return jnp.where(lower, a, roll(b, 16)), jnp.where(lower, roll(a, -16), b)


def sheet_update(water_ref, current_ref, surface_ref, sheet_ref):
    depth = water_ref.shape[0]

    def rows_of(block, carry):
        rows = pl.ds(pl.multiple_of(block * 8, 8), 8)
        surfaces = surface_ref[rows, :]
        water = [water_ref[k, rows, :] for k in range(depth)]
        drag = drag_rate * current_ref[rows, :]
        both = uptake(surfaces)
        inflow_anode = uptake_rate * (both[:, :64] - water[0])
        inflow_cathode = uptake_rate * (roll(both, 64)[:, :64] - water[depth - 1])
        for _ in range(SUBSTEPS):
            below = inflow_anode
            fresh = []
            for k in range(depth):
                if k < depth - 1:
                    mean = base_diffusion + (0.5 * slope_diffusion) * (water[k] + water[k + 1])
                    above = drag * water[k] - mean * (water[k + 1] - water[k])
                else:
                    above = -inflow_cathode
                fresh.append(water[k] + (below - above))
                below = above
            water = fresh
        for k in range(depth):
            sheet_ref[k, rows, :] = water[k]
        return carry

    lax.fori_loop(0, water_ref.shape[1] // 8, rows_of, 0)


def step_kernel(
    pop_hbm,
    mask_ref,
    water_ref,
    current_ref,
    out_ref,
    sheet_ref,
    raw,
    own,
    pack_low,
    pack_high,
    halo_low,
    halo_high,
    fields,
    mask,
    flux,
    psi,
    density,
    force,
    square,
    columns,
    send_pieces,
    recv_pieces,
    load_sem,
    send_sem,
    recv_sem,
    piece_send_sem,
    piece_recv_sem,
):
    side, gx, gy = lax.axis_index("side"), lax.axis_index("gx"), lax.axis_index("gy")
    gx_count, gy_count = lax.axis_size("gx"), lax.axis_size("gy")
    groups = 2 * gy_count
    me = side * gy_count + gy
    x_up = (side, lax.rem(gx + 1, gx_count), gy)
    x_down = (side, lax.rem(gx + gx_count - 1, gx_count), gy)
    y_up = (side, gx, lax.rem(gy + 1, gy_count))
    y_down = (side, gx, lax.rem(gy + gy_count - 1, gy_count))

    def peer(distance):
        other = lax.rem(me + distance, groups)
        return other, (other // gy_count, gx, lax.rem(other, gy_count))

    load = pltpu.make_async_copy(pop_hbm, raw, load_sem)
    load.start()
    barrier = pltpu.get_barrier_semaphore()
    for device in [x_up, x_down] + [peer(d)[1] for d in range(1, groups)]:
        pl.semaphore_signal(barrier, inc=1, device_id=device, device_id_type=MESH)

    copies = []

    def send(src, dst, device):
        slot = len(copies)
        copy = pltpu.make_async_remote_copy(
            src_ref=src,
            dst_ref=dst,
            send_sem=send_sem.at[slot],
            recv_sem=recv_sem.at[slot],
            device_id=device,
            device_id_type=MESH,
        )
        copy.start()
        copies.append(copy)
        return copy

    own[MASK_PLANE, 1:9] = jnp.swapaxes(
        mask_ref[...].astype(jnp.float32).reshape(128, 128), 0, 1
    ).reshape(8, 2, 8, 128)
    square[0:32, 0:64] = water_ref[0]
    square[32:64, 0:64] = water_ref[water_ref.shape[0] - 1]
    columns[...] = jnp.swapaxes(square[...], 0, 1)
    for s in range(2):
        faces = pack_columns(columns.at[pl.ds(0, 64)], 32 * s, 16)
        for g in range(8):
            send_pieces[s * 8 + g, 2:4, :] = faces[2 * g : 2 * g + 2]
    load.wait()
    total = None
    for i in range(LATTICE):
        turned = jnp.swapaxes(raw[i].reshape(128, 128), 0, 1)
        own[i, 1:9] = turned.reshape(8, 2, 8, 128)
    for i in range(LATTICE):
        part = own[i, 1:9].reshape(128, 128)
        total = part if total is None else total + part
    columns[...] = total
    surface = pack_columns(columns, 0, 32)
    for c in range(16):
        send_pieces[c, 0:2, :] = surface[2 * c : 2 * c + 2]
    pl.semaphore_wait(barrier, groups + 1)

    pieces = []
    for d in range(1, groups):
        other, device = peer(d)
        copy = pltpu.make_async_remote_copy(
            src_ref=send_pieces.at[other],
            dst_ref=recv_pieces.at[me],
            send_sem=piece_send_sem.at[d],
            recv_sem=piece_recv_sem.at[d],
            device_id=device,
            device_id_type=MESH,
        )
        copy.start()
        pieces.append(copy)
    main = pl.ds(0, LATTICE + 1)
    y_copies = [
        send(own.at[main, 8], own.at[main, 0], y_up),
        send(own.at[main, 1], own.at[main, 9], y_down),
    ]

    def pack_planes(i, carry):
        low, high = pack_pair(own[i, 1:9, 0], own[i, 1:9, 1])
        pack_low[i, 1:9] = low
        pack_high[i, 1:9] = high
        return carry

    lax.fori_loop(0, LATTICE + 1, pack_planes, 0)
    x_copies = [
        send(pack_low.at[main, pl.ds(1, 8)], halo_high.at[main, pl.ds(1, 8)], x_down),
        send(pack_high.at[main, pl.ds(1, 8)], halo_low.at[main, pl.ds(1, 8)], x_up),
    ]

    recv_pieces[me] = send_pieces[me]
    for copy in pieces:
        copy.wait()
    for c in range(16):
        square[2 * c : 2 * c + 2, :] = recv_pieces[c, 2:4, :]
        square[32 + 2 * c : 34 + 2 * c, :] = recv_pieces[c, 0:2, :]
    own_surface = columns[...]
    unpack_columns(square[0:32, :], columns)
    own_inflow = uptake_rate * (uptake(own_surface) - columns[...])
    own[FLUX_PLANE, 1:9] = own_inflow.reshape(8, 2, 8, 128)
    y_copies += [
        send(own.at[FLUX_PLANE, 8], own.at[FLUX_PLANE, 0], y_up),
        send(own.at[FLUX_PLANE, 1], own.at[FLUX_PLANE, 9], y_down),
    ]
    unpack_columns(square[32:64, :], columns)
    square[...] = jnp.swapaxes(columns[...], 0, 1)
    sheet_update(water_ref, current_ref, square, sheet_ref)

    for copy in y_copies:
        copy.wait()

    def pack_corners(i, carry):
        for t in (0, 9):
            low, high = pack_pair(own[i, t, 0], own[i, t, 1])
            pack_low[i, t] = low
            pack_high[i, t] = high
        return carry

    lax.fori_loop(0, LATTICE + 1, pack_corners, 0)
    low, high = pack_pair(own[FLUX_PLANE, :, 0], own[FLUX_PLANE, :, 1])
    pack_low[FLUX_PLANE] = low
    pack_high[FLUX_PLANE] = high
    for t in (0, 9):
        x_copies += [
            send(pack_low.at[main, t], halo_high.at[main, t], x_down),
            send(pack_high.at[main, t], halo_low.at[main, t], x_up),
        ]
    x_copies += [
        send(pack_low.at[FLUX_PLANE], halo_high.at[FLUX_PLANE], x_down),
        send(pack_high.at[FLUX_PLANE], halo_low.at[FLUX_PLANE], x_up),
    ]
    for copy in x_copies:
        copy.wait()

    lane = lanes_of((8, 128))
    first = lane < 64
    last = lane >= 64
    is_low = lane % 64 < 16
    is_high = lane % 64 >= 48

    def assemble(t, carry):
        start = pl.multiple_of(t * 16 + PAD, 8)
        for i in range(PLANES):
            a, b = own[i, t, 0], own[i, t, 1]
            low, high = halo_low[i, t], halo_high[i, t]

            def join(middle, left, right):
                return jnp.where(is_low, left, jnp.where(is_high, right, middle))

            tiles = (
                (join(roll(a, 16), low, roll(high, 48)), join(roll(b, 16), roll(low, -16), roll(high, 32))),
                (
                    join(roll(a, -16), roll(low, -32), roll(high, 16)),
                    join(roll(b, -16), roll(low, -48), high),
                ),
            )
            for k in range(2):
                if i < LATTICE:
                    shift = velocity_table[i][1]
                    fields[0, i, 0, pl.ds(start + 8 * k - shift, 8), :] = tiles[0][k]
                    fields[0, i, 1, pl.ds(start + 8 * k - shift, 8), :] = tiles[1][k]
                elif i == MASK_PLANE:
                    mask[0, pl.ds(start + 8 * k, 8), :] = tiles[0][k]
                    mask[1, pl.ds(start + 8 * k, 8), :] = tiles[1][k]
                else:
                    flux[pl.ds(start + 8 * k, 8), :] = tiles[0][k]
        return carry

    lax.fori_loop(0, PAIRS, assemble, 0)

    zero = jnp.zeros((8, 128), jnp.float32)

    def layers_sum(a, b):
        return (
            b + jnp.where(last, roll(b, 64), zero),
            a + jnp.where(first, roll(a, 64), zero),
        )

    def layers_difference(a, b):
        return (
            b - jnp.where(last, roll(b, 64), zero),
            jnp.where(first, roll(a, 64), zero) - a,
        )

    def load_fields(now, group, start):
        return [
            fields[now, i, group, pl.ds(start - velocity_table[i][1], 8), :] for i in range(LATTICE)
        ]

    def potentials(now, start):
        for group in range(2):
            loaded = load_fields(now, group, start)
            while len(loaded) > 1:
                loaded = [
                    loaded[k] + loaded[k + 1] if k + 1 < len(loaded) else loaded[k]
                    for k in range(0, len(loaded), 2)
                ]
            rho = loaded[0]
            rows = pl.ds(start, 8)
            density[group, rows, :] = rho
            psi[group, rows, :] = jnp.where(
                mask[group, rows, :] > 0.5, 1.0 - jnp.exp(-rho), wall_potential
            )

    def forces(start):
        centre = [psi[g, pl.ds(start, 8), :] for g in range(2)]
        above = [psi[g, pl.ds(start + 1, 8), :] for g in range(2)]
        below = [psi[g, pl.ds(start - 1, 8), :] for g in range(2)]
        slope = [above[g] - below[g] for g in range(2)]
        base = [(centre[g] + centre[g]) + (above[g] + below[g]) for g in range(2)]
        layers = layers_sum(*centre)
        along_x = [base[g] + layers[g] for g in range(2)]
        slope_layers = layers_sum(*slope)
        along_z = layers_difference(
            *[base[g] + (roll(centre[g], 1) + roll(centre[g], -1)) for g in range(2)]
        )
        scale = 3.0 * KAPPA * relax_time * -coupling / 36.0
        for g in range(2):
            factor = scale * centre[g]
            rows = pl.ds(start, 8)
            force[0, g, rows, :] = factor * (roll(along_x[g], -1) - roll(along_x[g], 1))
            force[1, g, rows, :] = factor * (
                (slope[g] + slope[g]) + slope_layers[g] + (roll(slope[g], 1) + roll(slope[g], -1))
            )
            force[2, g, rows, :] = factor * along_z[g]

    def collide(now, group, start):
        rows = pl.ds(start, 8)
        f = load_fields(now, group, start)
        rho = density[group, rows, :]
        inverse = 1.0 / rho
        odd = [None] + [f[i] - f[i + 1] for i in range(1, LATTICE, 2)]
        moment = (
            odd[1] + odd[4] + odd[5] + (odd[6] + odd[7]),
            odd[2] + odd[4] - odd[5] + (odd[8] + odd[9]),
            odd[3] + odd[6] - odd[7] + (odd[8] - odd[9]),
        )
        flow = [(3.0 * KAPPA) * moment[c] + force[c, group, rows, :] for c in range(3)]
        speed = flow[0] * flow[0] + flow[1] * flow[1] + flow[2] * flow[2]
        scaled = (0.5 / KAPPA) * inverse
        base = KAPPA * rho - (1.5 * KAPPA / (9.0 * KAPPA * KAPPA)) * (speed * inverse)
        double = base + base
        is_pore = mask[group, rows, :] > 0.5
        post = [None] * LATTICE
        post[0] = jnp.where(is_pore, 12.0 * base - (RATE - 1.0) * f[0], f[0])
        for i in range(1, LATTICE, 2):
            velocity = velocity_table[i]
            along = None
            for c in range(3):
                if velocity[c] == 0:
                    continue
                if along is None:
                    along = flow[c]
                elif velocity[c] > 0:
                    along = along + flow[c]
                else:
                    along = along - flow[c]
            if i < 7:
                twice = along + along
                even = double + twice * (along * scaled)
                along = twice
            else:
                even = base + along * (along * scaled)
            up = (even + along) - (RATE - 1.0) * f[i]
            down = (even - along) - (RATE - 1.0) * f[i + 1]
            post[i] = jnp.where(is_pore, up, f[i + 1])
            post[i + 1] = jnp.where(is_pore, down, f[i])
        return post

    def collide_and_move(now, start):
        then = 1 - now
        rows = pl.ds(start, 8)
        a = collide(now, 0, start)
        b = collide(now, 1, start)
        wall_flux = flux[rows, :]
        wall_pair = {1.0 / 18.0: (6.0 / 18.0) * wall_flux, 1.0 / 36.0: (6.0 / 36.0) * wall_flux}
        for i in range(LATTICE):
            shift_x, shift_y, shift_z = velocity_table[i]
            moved = pl.ds(start - shift_y, 8)
            if shift_z == 0:
                fields[then, i, 0, rows, :] = roll(a[i], shift_x)
                fields[then, i, 1, rows, :] = roll(b[i], shift_x)
            elif shift_z == 1:
                fields[then, i, 1, rows, :] = roll(a[i], shift_x)
                wall = a[opposite_index[i]] - wall_pair[weight_table[i]]
                inner = roll(b[i], 64 + shift_x)
                if shift_y == 0:
                    fields[then, i, 0, rows, :] = jnp.where(last, inner, wall)
                else:
                    pltpu.store(fields.at[then, i, 0, rows, :], inner, mask=last)
                    pltpu.store(fields.at[then, i, 0, moved, :], wall, mask=first)
            else:
                fields[then, i, 0, rows, :] = roll(b[i], shift_x)
                wall = b[opposite_index[i]]
                inner = roll(a[i], 64 + shift_x)
                if shift_y == 0:
                    fields[then, i, 1, rows, :] = jnp.where(first, inner, wall)
                else:
                    pltpu.store(fields.at[then, i, 1, rows, :], inner, mask=first)
                    pltpu.store(fields.at[then, i, 1, moved, :], wall, mask=last)

    def one_step(step, carry):
        now = lax.rem(step, 2)
        skip = step // 4
        begin = skip * 8 + PAD
        tiles = 2 * PAIRS - 2 * skip

        def start_of(t):
            return pl.multiple_of(begin + t * 8, 8)

        def potential_pass(t, c):
            for k in range(2):
                potentials(now, start_of(2 * t + k))
            return c

        def force_pass(t, c):
            for k in range(2):
                forces(start_of(2 * t + k))
            return c

        def move_pass(t, c):
            collide_and_move(now, start_of(t))
            return c

        lax.fori_loop(0, tiles // 2, potential_pass, 0)
        lax.fori_loop(0, tiles // 2, force_pass, 0)
        lax.fori_loop(0, tiles, move_pass, 0)
        return carry

    lax.fori_loop(0, STEPS, one_step, 0)

    even_layer = lanes_of((128, 128)) // 32 % 2 == 0
    for i in range(LATTICE):
        rows = pl.ds(PAD + 16 - velocity_table[i][1], 128)
        a, b = fields[STEPS % 2, i, 0, rows, :], fields[STEPS % 2, i, 1, rows, :]
        merged = jnp.where(even_layer, roll(a, -16), roll(b, 16))
        out_ref[i] = jnp.swapaxes(merged, 0, 1).reshape(4, 32, 128)


def on_device(populations, solid_mask, water_sheet, current):
    vmem = pl.BlockSpec(memory_space=pltpu.VMEM)
    lattice, water = pl.pallas_call(
        step_kernel,
        out_shape=(
            jax.ShapeDtypeStruct(populations.shape[1:], jnp.float32),
            jax.ShapeDtypeStruct(water_sheet.shape, jnp.float32),
        ),
        in_specs=[pl.BlockSpec(memory_space=pl.ANY), vmem, vmem, vmem],
        out_specs=(vmem, vmem),
        scratch_shapes=[
            pltpu.VMEM((LATTICE, 4, 32, 128), jnp.float32),
            pltpu.VMEM((PLANES, PAIRS, 2, 8, 128), jnp.float32),
            pltpu.VMEM((PLANES, PAIRS, 8, 128), jnp.float32),
            pltpu.VMEM((PLANES, PAIRS, 8, 128), jnp.float32),
            pltpu.VMEM((PLANES, PAIRS, 8, 128), jnp.float32),
            pltpu.VMEM((PLANES, PAIRS, 8, 128), jnp.float32),
            pltpu.VMEM((2, LATTICE, 2, ROWS, 128), jnp.float32),
            pltpu.VMEM((2, ROWS, 128), jnp.float32),
            pltpu.VMEM((ROWS, 128), jnp.float32),
            pltpu.VMEM((2, ROWS, 128), jnp.float32),
            pltpu.VMEM((2, ROWS, 128), jnp.float32),
            pltpu.VMEM((3, 2, ROWS, 128), jnp.float32),
            pltpu.VMEM((128, 128), jnp.float32),
            pltpu.VMEM((128, 128), jnp.float32),
            pltpu.VMEM((16, 4, 128), jnp.float32),
            pltpu.VMEM((16, 4, 128), jnp.float32),
            pltpu.SemaphoreType.DMA,
            pltpu.SemaphoreType.DMA((12,)),
            pltpu.SemaphoreType.DMA((12,)),
            pltpu.SemaphoreType.DMA((16,)),
            pltpu.SemaphoreType.DMA((16,)),
        ],
        compiler_params=pltpu.CompilerParams(
            collective_id=0, has_side_effects=True, vmem_limit_bytes=48 * 1024 * 1024
        ),
    )(populations[0], solid_mask[0], water_sheet, current)
    return (lattice[None], water)


def solution(mesh):
    in_specs = (
        P("side", None, None, "gx", "gy"),
        P("side", None, "gx", "gy"),
        P(None, "gx", ("side", "gy")),
        P("gx", ("side", "gy")),
    )
    out_specs = (P("side", None, None, "gx", "gy"), P(None, "gx", ("side", "gy")))
    return jax.shard_map(
        on_device, mesh=mesh, in_specs=in_specs, out_specs=out_specs, check_vma=False
    )
```

profile of v0, /device:TPU:1, one launch (start us, length us, event | category | flops | bytes accessed | tf_op | source)
XLA Modules:
  0.0 71.1 jit_solution(7503778779001243104)
XLA Ops:
  0.6 0.0 copy-start
  0.6 1.3 %copy-done = f32[1,19,4,32,128]{4,3,2,1,0:T(8,128)S(1)} copy-done((f32[1,19,4,32,128]{4,3,2,1,0:T(8,128)S(1)}, f32[1,19,4,32,128]{4,3,2,1,0:T(8,128)}, u32[]{:S(2)}) %copy-start) | copy-done | bytes 1245208
  1.9 0.0 copy-start.1
  1.9 1.0 %copy-done.1 = f32[32,32,64]{2,1,0:T(8,128)S(1)} copy-done((f32[32,32,64]{2,1,0:T(8,128)S(1)}, f32[32,32,64]{2,1,0:T(8,128)}, u32[]{:S(2)}) %copy-start.1) | copy-done | bytes 262168
  3.0 0.0 copy-start.2
  3.0 0.8 %copy-done.2 = s32[1,4,32,128]{3,2,1,0:T(8,128)S(1)} copy-done((s32[1,4,32,128]{3,2,1,0:T(8,128)S(1)}, s32[1,4,32,128]{3,2,1,0:T(8,128)}, u32[]{:S(2)}) %copy-start.2) | copy-done | bytes 65560
  3.8 0.0 copy-start.3
  3.8 0.7 %copy-done.3 = f32[32,64]{1,0:T(8,128)S(1)} copy-done((f32[32,64]{1,0:T(8,128)S(1)}, f32[32,64]{1,0:T(8,128)}, u32[]{:S(2)}) %copy-start.3) | copy-done | bytes 8216
  4.5 64.7 %shard_map.59 = (f32[19,4,32,128]{3,2,1,0:T(8,128)S(1)}, f32[32,32,64]{2,1,0:T(8,128)S(1)}) custom-call(f32[19,4,32,128]{3,2,1,0:T(8,128)S(1)} %bitcast.3, s32[4,32,128]{2,1,0:T(8,128)S(1)} %bitcast.5, f32[32,32,64]{2,1,0:T(8,128)S(1)} %copy-done.1, f32[32,64]{1,0:T(8,128)S(1)} %copy-done.3), custom_call_target="tpu_custom_call" | custom-call | tf_op jit(solution)/shard_map/pallas_call | solution.py:491
  69.2 1.0 %copy.8 = f32[1,19,4,32,128]{4,3,2,1,0:T(8,128)} copy(f32[1,19,4,32,128]{4,3,2,1,0:T(8,128)S(1)} %bitcast.4) | data formatting | bytes 2490368
  70.3 0.8 %copy.9 = f32[32,32,64]{2,1,0:T(8,128)} copy(f32[32,32,64]{2,1,0:T(8,128)S(1)} %get-tuple-element.9) | data formatting | bytes 524288
Async XLA Ops:
  0.6 1.3 %copy-start = (f32[1,19,4,32,128]{4,3,2,1,0:T(8,128)S(1)}, f32[1,19,4,32,128]{4,3,2,1,0:T(8,128)}, u32[]{:S(2)}) copy-start(f32[1,19,4,32,128]{4,3,2,1,0:T(8,128)} %param.4) | copy-start | bytes 3735556
  1.9 1.0 %copy-start.1 = (f32[32,32,64]{2,1,0:T(8,128)S(1)}, f32[32,32,64]{2,1,0:T(8,128)}, u32[]{:S(2)}) copy-start(f32[32,32,64]{2,1,0:T(8,128)} %water_ref.1) | copy-start | bytes 786436
  3.0 0.8 %copy-start.2 = (s32[1,4,32,128]{3,2,1,0:T(8,128)S(1)}, s32[1,4,32,128]{3,2,1,0:T(8,128)}, u32[]{:S(2)}) copy-start(s32[1,4,32,128]{3,2,1,0:T(8,128)} %param.5) | copy-start | bytes 196612
  3.8 0.7 %copy-start.3 = (f32[32,64]{1,0:T(8,128)S(1)}, f32[32,64]{1,0:T(8,128)}, u32[]{:S(2)}) copy-start(f32[32,64]{1,0:T(8,128)} %current_ref.1) | copy-start | bytes 24580
where the time goes:
time: 71.4 us; the launch traced here: 71.1 us
  Pallas kernels  64.7 us (91%)
  local copies, waits for them, and re-layouts  5.71 us (8%)
    pallas_call x1, Pallas kernels, on_device(): pl.pallas_call(step_kernel, out_shape=(jax.ShapeDtypeStruct(populations.s...  64.7 us
    unnamed x10, local copies, waits for them, and re-layouts  5.71 us

commit v1 on v0

v1 whole, which is shorter than its diff:
```python
import functools

import jax
import jax.numpy as jnp
from jax import lax
from jax.experimental import pallas as pl
from jax.experimental.pallas import tpu as pltpu
from jax.sharding import PartitionSpec as P

STEPS = 8
SUBSTEPS = 2
LATTICE = 19
MESH = pl.DeviceIdType.MESH

velocity_table = (
    (0, 0, 0),
    (1, 0, 0),
    (-1, 0, 0),
    (0, 1, 0),
    (0, -1, 0),
    (0, 0, 1),
    (0, 0, -1),
    (1, 1, 0),
    (-1, -1, 0),
    (1, -1, 0),
    (-1, 1, 0),
    (1, 0, 1),
    (-1, 0, -1),
    (1, 0, -1),
    (-1, 0, 1),
    (0, 1, 1),
    (0, -1, -1),
    (0, 1, -1),
    (0, -1, 1),
)
opposite_index = (0, 2, 1, 4, 3, 6, 5, 8, 7, 10, 9, 12, 11, 14, 13, 16, 15, 18, 17)
weight_table = (1.0 / 3.0,) + (1.0 / 18.0,) * 6 + (1.0 / 36.0,) * 12
relax_time = 0.8
coupling = -3.0
wall_potential = 0.4
uptake_rate = 0.02
drag_rate = 0.03
base_diffusion = 0.05
slope_diffusion = 0.015

PAIRS = 10
PAD = 8
ROWS = 16 * PAIRS + 2 * PAD
MASK_PLANE = LATTICE
FLUX_PLANE = LATTICE + 1
PLANES = LATTICE + 2
RATE = 1.0 / relax_time
KAPPA = RATE / 36.0


def roll(values, shift):
    shift = shift % 128
    if shift == 0:
        return values
    return pltpu.roll(values, shift, values.ndim - 1)


def lanes_of(shape):
    return lax.broadcasted_iota(jnp.int32, shape, len(shape) - 1)


def uptake(density_row):
    activity = density_row / (1.0 + density_row)
    return 0.043 + activity * (17.18 + activity * (-39.85 + 36.0 * activity))


def pack_columns(ref, offset, rows):
    lanes = lanes_of((rows, 128))
    packed = None
    for m in range(4):
        part = roll(ref[pl.ds(m, rows, stride=4), :], 32 * m - offset)
        packed = part if packed is None else jnp.where(lanes >= 32 * m, part, packed)
    return packed


def unpack_columns(packed, ref):
    for m in range(4):
        ref[pl.ds(m, packed.shape[0], stride=4), :] = roll(packed, -32 * m)


def pack_pair(a, b):
    lower = lanes_of(a.shape) % 32 < 16
    return jnp.where(lower, a, roll(b, 16)), jnp.where(lower, roll(a, -16), b)


def sheet_update(water_ref, current_ref, surface_ref, sheet_ref):
    depth = water_ref.shape[0]

    def rows_of(block, carry):
        rows = pl.ds(pl.multiple_of(block * 8, 8), 8)
        surfaces = surface_ref[rows, :]
        water = [water_ref[k, rows, :] for k in range(depth)]
        drag = drag_rate * current_ref[rows, :]
        both = uptake(surfaces)
        inflow_anode = uptake_rate * (both[:, :64] - water[0])
        inflow_cathode = uptake_rate * (roll(both, 64)[:, :64] - water[depth - 1])
        for _ in range(SUBSTEPS):
            below = inflow_anode
            fresh = []
            for k in range(depth):
                if k < depth - 1:
                    mean = base_diffusion + (0.5 * slope_diffusion) * (water[k] + water[k + 1])
                    above = drag * water[k] - mean * (water[k + 1] - water[k])
                else:
                    above = -inflow_cathode
                fresh.append(water[k] + (below - above))
                below = above
            water = fresh
        for k in range(depth):
            sheet_ref[k, rows, :] = water[k]
        return carry

    lax.fori_loop(0, water_ref.shape[1] // 8, rows_of, 0)


def step_kernel(
    pop_hbm,
    mask_hbm,
    water_hbm,
    current_hbm,
    out_ref,
    sheet_ref,
    raw,
    raw_mask,
    water_ref,
    current_ref,
    own,
    pack_low,
    pack_high,
    halo_low,
    halo_high,
    fields_even,
    fields_odd,
    coefficients,
    flux,
    slopes,
    centres,
    stage,
    square,
    columns,
    send_pieces,
    recv_pieces,
    load_sem,
    send_sem,
    recv_sem,
    piece_send_sem,
    piece_recv_sem,
):
    side, gx, gy = lax.axis_index("side"), lax.axis_index("gx"), lax.axis_index("gy")
    gx_count, gy_count = lax.axis_size("gx"), lax.axis_size("gy")
    groups = 2 * gy_count
    me = side * gy_count + gy
    x_up = (side, lax.rem(gx + 1, gx_count), gy)
    x_down = (side, lax.rem(gx + gx_count - 1, gx_count), gy)
    y_up = (side, gx, lax.rem(gy + 1, gy_count))
    y_down = (side, gx, lax.rem(gy + gy_count - 1, gy_count))

    def peer(distance):
        other = lax.rem(me + distance, groups)
        return other, (other // gy_count, gx, lax.rem(other, gy_count))

    barrier = pltpu.get_barrier_semaphore()
    for device in [x_up, x_down] + [peer(d)[1] for d in range(1, groups)]:
        pl.semaphore_signal(barrier, inc=1, device_id=device, device_id_type=MESH)
    loads = [
        pltpu.make_async_copy(source, target, load_sem.at[k])
        for k, (source, target) in enumerate(
            ((pop_hbm, raw), (mask_hbm, raw_mask), (water_hbm, water_ref), (current_hbm, current_ref))
        )
    ]
    for load in loads:
        load.start()

    copies = []

    def send(src, dst, device):
        slot = len(copies)
        copy = pltpu.make_async_remote_copy(
            src_ref=src,
            dst_ref=dst,
            send_sem=send_sem.at[slot],
            recv_sem=recv_sem.at[slot],
            device_id=device,
            device_id_type=MESH,
        )
        copy.start()
        copies.append(copy)
        return copy

    loads[0].wait()
    for i in range(LATTICE):
        turned = jnp.swapaxes(raw[i].reshape(128, 128), 0, 1)
        own[i, 1:9] = turned.reshape(8, 2, 8, 128)
    loads[1].wait()
    own[MASK_PLANE, 1:9] = jnp.swapaxes(
        raw_mask[...].astype(jnp.float32).reshape(128, 128), 0, 1
    ).reshape(8, 2, 8, 128)
    loads[2].wait()
    loads[3].wait()
    square[0:32, 0:64] = water_ref[0]
    square[32:64, 0:64] = water_ref[water_ref.shape[0] - 1]
    columns[...] = jnp.swapaxes(square[...], 0, 1)
    for s in range(2):
        faces = pack_columns(columns.at[pl.ds(0, 64)], 32 * s, 16)
        for g in range(8):
            send_pieces[s * 8 + g, 2:4, :] = faces[2 * g : 2 * g + 2]
    total = None
    for i in range(LATTICE):
        part = own[i, 1:9].reshape(128, 128)
        total = part if total is None else total + part
    columns[...] = total
    surface = pack_columns(columns, 0, 32)
    for c in range(16):
        send_pieces[c, 0:2, :] = surface[2 * c : 2 * c + 2]
    main = pl.ds(0, LATTICE + 1)
    inner = pl.ds(1, 8)

    def pack_planes(i):
        low, high = pack_pair(own[i, 1:9, 0], own[i, 1:9, 1])
        pack_low[i, 1:9] = low
        pack_high[i, 1:9] = high

    def pack_four(k, carry):
        for i in range(4):
            pack_planes(4 * k + i)
        return carry

    lax.fori_loop(0, (LATTICE + 1) // 4, pack_four, 0)
    pl.semaphore_wait(barrier, groups + 1)
    pieces = []
    for d in range(1, groups):
        other, device = peer(d)
        copy = pltpu.make_async_remote_copy(
            src_ref=send_pieces.at[other],
            dst_ref=recv_pieces.at[me],
            send_sem=piece_send_sem.at[d],
            recv_sem=piece_recv_sem.at[d],
            device_id=device,
            device_id_type=MESH,
        )
        copy.start()
        pieces.append(copy)

    y_copies = [
        send(own.at[main, 8], own.at[main, 0], y_up),
        send(own.at[main, 1], own.at[main, 9], y_down),
    ]
    x_copies = [
        send(pack_low.at[main, inner], halo_high.at[main, inner], x_down),
        send(pack_high.at[main, inner], halo_low.at[main, inner], x_up),
    ]

    lane = lanes_of((8, 128))
    first = lane < 64
    last = lane >= 64
    is_low = lane % 64 < 16
    is_high = lane % 64 >= 48

    def planes_at(t, planes):
        start = pl.multiple_of(t * 16 + PAD, 8)
        for i in planes:
            for k in range(2):
                rows = pl.ds(start + 8 * k, 8)
                if i < LATTICE:
                    moved = pl.ds(start + 8 * k - velocity_table[i][1], 8)
                    yield i, k, [fields_even.at[0, i, g, moved, :] for g in range(2)]
                elif i == MASK_PLANE:
                    yield i, k, [coefficients.at[0, g, rows, :] for g in range(2)]
                else:
                    yield i, k, [flux.at[rows, :], None]

    def place_own(t, planes):
        for i, k, targets in planes_at(t, planes):
            tile = own[i, t, k]
            for target, shift in zip(targets, (16, -16)):
                if target is not None:
                    target[...] = roll(tile, shift)

    def place_halo(t):
        for i, k, targets in planes_at(t, range(PLANES)):
            low, high = halo_low[i, t], halo_high[i, t]
            for g, target in enumerate(targets):
                if target is not None:
                    pltpu.store(target, roll(low, -16 * k - 32 * g), mask=is_low)
                    pltpu.store(target, roll(high, 48 - 16 * k - 32 * g), mask=is_high)
        start = pl.multiple_of(t * 16 + PAD, 8)
        for k in range(2):
            rows = pl.ds(start + 8 * k, 8)
            for g in range(2):
                pore = coefficients[0, g, rows, :]
                coefficients[1, g, rows, :] = (3.0 * KAPPA) * pore
                coefficients[2, g, rows, :] = (0.5 + 0.5 * (RATE - 1.0)) * pore - 0.5
                coefficients[3, g, rows, :] = 0.5 - (0.5 - 0.5 * (RATE - 1.0)) * pore
                coefficients[4, g, rows, :] = 1.0 - RATE * pore

    def place_inner(t, carry):
        place_own(t, range(LATTICE + 1))
        return carry

    lax.fori_loop(1, 9, place_inner, 0)

    recv_pieces[me] = send_pieces[me]
    for copy in pieces:
        copy.wait()
    for c in range(16):
        square[2 * c : 2 * c + 2, :] = recv_pieces[c, 2:4, :]
        square[32 + 2 * c : 34 + 2 * c, :] = recv_pieces[c, 0:2, :]
    own_surface = columns[...]
    unpack_columns(square[0:32, :], columns)
    own_inflow = uptake_rate * (uptake(own_surface) - columns[...])
    own[FLUX_PLANE, 1:9] = own_inflow.reshape(8, 2, 8, 128)
    y_copies += [
        send(own.at[FLUX_PLANE, 8], own.at[FLUX_PLANE, 0], y_up),
        send(own.at[FLUX_PLANE, 1], own.at[FLUX_PLANE, 9], y_down),
    ]
    pack_planes(FLUX_PLANE)
    x_copies += [
        send(pack_low.at[FLUX_PLANE, inner], halo_high.at[FLUX_PLANE, inner], x_down),
        send(pack_high.at[FLUX_PLANE, inner], halo_low.at[FLUX_PLANE, inner], x_up),
    ]
    unpack_columns(square[32:64, :], columns)
    square[...] = jnp.swapaxes(columns[...], 0, 1)
    sheet_update(water_ref, current_ref, square, sheet_ref)

    for t in range(1, 9):
        place_own(t, [FLUX_PLANE])
    for copy in y_copies:
        copy.wait()

    def pack_corners(k, carry):
        for i in range(3):
            for t in (0, 9):
                low, high = pack_pair(own[3 * k + i, t, 0], own[3 * k + i, t, 1])
                pack_low[3 * k + i, t] = low
                pack_high[3 * k + i, t] = high
        return carry

    lax.fori_loop(0, PLANES // 3, pack_corners, 0)
    corner_copies = []
    for t in (0, 9):
        corner_copies += [
            send(pack_low.at[:, t], halo_high.at[:, t], x_down),
            send(pack_high.at[:, t], halo_low.at[:, t], x_up),
        ]

    for t in (0, 9):
        place_own(t, range(PLANES))

    zero = jnp.zeros((8, 128), jnp.float32)

    def layers_sum(a, b, a_turned, b_turned):
        return b + jnp.where(last, b_turned, zero), a + jnp.where(first, a_turned, zero)

    def layers_difference(a, b, a_turned, b_turned):
        return b - jnp.where(last, b_turned, zero), jnp.where(first, a_turned, zero) - a

    def load_fields(fields, group, start):
        return [
            fields[i, group, pl.ds(start - velocity_table[i][1], 8), :] for i in range(LATTICE)
        ]

    def potentials(fields, slopes, start):
        rows = pl.ds(start, 8)
        potential = []
        for g in range(2):
            loaded = load_fields(fields, g, start)
            while len(loaded) > 1:
                loaded = [
                    loaded[k] + loaded[k + 1] if k + 1 < len(loaded) else loaded[k]
                    for k in range(0, len(loaded), 2)
                ]
            rho = loaded[0]
            pore = coefficients[0, g, rows, :]
            is_pore = pore > 0.5
            value = jnp.where(is_pore, 1.0 - jnp.exp(-rho), wall_potential)
            potential.append(value)
            centres[0, g, rows, :] = (KAPPA * pore) * rho
            centres[1, g, rows, :] = (0.5 / KAPPA) / rho
            centres[2, g, rows, :] = (3.0 * KAPPA * relax_time * -coupling / 36.0) * (pore * value)
        right = [roll(p, -1) for p in potential]
        left = [roll(p, 1) for p in potential]
        turned = [roll(p, 64) for p in potential]
        right_turned = [roll(p, 63) for p in potential]
        left_turned = [roll(p, 65) for p in potential]
        slope_x = [right[g] - left[g] for g in range(2)]
        slope_x_turned = [right_turned[g] - left_turned[g] for g in range(2)]
        wide = [(potential[g] + potential[g]) + (right[g] + left[g]) for g in range(2)]
        wide_turned = [(turned[g] + turned[g]) + (right_turned[g] + left_turned[g]) for g in range(2)]
        layers = layers_sum(*potential, *turned)
        slope_z = layers_difference(*potential, *turned)
        slope_x_layers = layers_sum(*slope_x, *slope_x_turned)
        slope_z_wide = layers_difference(*wide, *wide_turned)
        for g in range(2):
            slopes[0, g, rows, :] = slope_x[g]
            slopes[1, g, rows, :] = wide[g] + layers[g]
            slopes[2, g, rows, :] = slope_z[g]
            centres[3, g, rows, :] = (slope_x[g] + slope_x[g]) + slope_x_layers[g]
            centres[4, g, rows, :] = slope_z_wide[g]

    def collide(fields, slopes, g, start):
        rows = pl.ds(start, 8)
        above, below = pl.ds(start + 1, 8), pl.ds(start - 1, 8)
        f = load_fields(fields, g, start)
        odd = [None] + [f[i] - f[i + 1] for i in range(1, LATTICE, 2)]
        sums = [None] + [f[i] + f[i + 1] for i in range(1, LATTICE, 2)]
        moment = (
            (odd[1] + odd[4]) + (odd[5] + (odd[6] + odd[7])),
            (odd[2] + odd[4]) + ((odd[8] + odd[9]) - odd[5]),
            (odd[3] + odd[6]) + ((odd[8] - odd[9]) - odd[7]),
        )
        gradient = (
            centres[3, g, rows, :] + (slopes[0, g, above, :] + slopes[0, g, below, :]),
            slopes[1, g, above, :] - slopes[1, g, below, :],
            centres[4, g, rows, :] + (slopes[2, g, above, :] + slopes[2, g, below, :]),
        )
        factor = centres[2, g, rows, :]
        three = coefficients[1, g, rows, :]
        even_part = coefficients[2, g, rows, :]
        odd_part = coefficients[3, g, rows, :]
        flow = [three * moment[c] + factor * gradient[c] for c in range(3)]
        speed = flow[0] * flow[0] + flow[1] * flow[1] + flow[2] * flow[2]
        scaled = centres[1, g, rows, :]
        base = centres[0, g, rows, :] - (1.0 / 3.0) * (speed * scaled)
        double = base + base
        post = [None] * LATTICE
        post[0] = 12.0 * base + coefficients[4, g, rows, :] * f[0]
        for p in range(1, 10):
            i = 2 * p - 1
            velocity = velocity_table[i]
            along = None
            for c in range(3):
                if velocity[c] == 0:
                    continue
                if along is None:
                    along = flow[c]
                elif velocity[c] > 0:
                    along = along + flow[c]
                else:
                    along = along - flow[c]
            if i < 7:
                twice = along + along
                even = double + twice * (along * scaled)
                along = twice
            else:
                even = base + along * (along * scaled)
            even = even - even_part * sums[p]
            along = along - odd_part * odd[p]
            post[i] = even + along
            post[i + 1] = even - along
        return post

    def relax(fields, slopes, start, half):
        a = collide(fields, slopes, 0, start)
        b = collide(fields, slopes, 1, start)
        wall_flux = flux[pl.ds(start, 8), :]
        walls = 0
        for i in range(LATTICE):
            stage[half, i] = a[i]
            stage[half, LATTICE + i] = b[i]
            if velocity_table[i][2] == 1:
                stage[half, 2 * LATTICE + walls] = (
                    a[opposite_index[i]] - (6.0 * weight_table[i]) * wall_flux
                )
                walls += 1

    def move(fields, start, half):
        rows = pl.ds(start, 8)
        walls = 0
        for i in range(LATTICE):
            shift_x, shift_y, shift_z = velocity_table[i]
            moved = pl.ds(start - shift_y, 8)
            a, b = stage[half, i], stage[half, LATTICE + i]
            if shift_z == 0:
                fields[i, 0, rows, :] = roll(a, shift_x)
                fields[i, 1, rows, :] = roll(b, shift_x)
            elif shift_z == 1:
                fields[i, 1, rows, :] = roll(a, shift_x)
                pltpu.store(fields.at[i, 0, rows, :], roll(b, 64 + shift_x), mask=last)
                wall = stage[half, 2 * LATTICE + walls]
                pltpu.store(fields.at[i, 0, moved, :], wall, mask=first)
                walls += 1
            else:
                fields[i, 0, rows, :] = roll(b, shift_x)
                pltpu.store(fields.at[i, 1, rows, :], roll(a, 64 + shift_x), mask=first)
                wall = stage[half, LATTICE + opposite_index[i]]
                pltpu.store(fields.at[i, 1, moved, :], wall, mask=last)

    def run_steps(tiles, begin, end):
        starts = [tile * 8 + PAD for tile in tiles]

        def one_step(step, now, then):
            for start in starts:
                potentials(now, slopes.at[step], start)
            for slot, start in enumerate(starts):
                relax(now, slopes.at[step], start, slot)
                if slot % 2 == 1 and slot > 2:
                    for done in (slot - 3, slot - 2):
                        move(then, starts[done], done)
            for done in (len(starts) - 2, len(starts) - 1):
                move(then, starts[done], done)

        def two_steps(half, carry):
            one_step(2 * half, fields_even.at[half], fields_odd.at[half])
            one_step(2 * half + 1, fields_odd.at[half], fields_even.at[half + 1])
            return carry

        lax.fori_loop(begin // 2, end // 2, two_steps, 0)

    for copy in x_copies:
        copy.wait()

    def halo_inner(t, carry):
        place_halo(t)
        return carry

    lax.fori_loop(1, 9, halo_inner, 0)
    run_steps(range(2, 18), 0, STEPS)
    for copy in corner_copies:
        copy.wait()
    for t in (0, 9):
        place_halo(t)
    for base in range(2):
        ends = [base + k for k in range(3)] + [17 - base + k for k in range(3)]
        run_steps(ends, base * STEPS // 2, (base + 1) * STEPS // 2)

    even_layer = lanes_of((128, 128)) // 32 % 2 == 0
    for i in range(LATTICE):
        rows = pl.ds(PAD + 16 - velocity_table[i][1], 128)
        a, b = fields_even[STEPS // 2, i, 0, rows, :], fields_even[STEPS // 2, i, 1, rows, :]
        merged = jnp.where(even_layer, roll(a, -16), roll(b, 16))
        out_ref[i] = jnp.swapaxes(merged, 0, 1).reshape(4, 32, 128)


def on_device(populations, solid_mask, water_sheet, current):
    arguments = (populations[0], solid_mask[0], water_sheet, current)
    vmem = pl.BlockSpec(memory_space=pltpu.VMEM)
    hbm = pl.BlockSpec(memory_space=pltpu.HBM)
    lattice, water = pl.pallas_call(
        step_kernel,
        out_shape=(
            jax.ShapeDtypeStruct(populations.shape[1:], jnp.float32),
            jax.ShapeDtypeStruct(water_sheet.shape, jnp.float32),
        ),
        in_specs=[hbm, hbm, hbm, hbm],
        out_specs=(vmem, vmem),
        scratch_shapes=[
            pltpu.VMEM((LATTICE, 4, 32, 128), jnp.float32),
            pltpu.VMEM(solid_mask.shape[1:], jnp.int32),
            pltpu.VMEM(water_sheet.shape, jnp.float32),
            pltpu.VMEM(current.shape, jnp.float32),
            pltpu.VMEM((PLANES, PAIRS, 2, 8, 128), jnp.float32),
            pltpu.VMEM((PLANES, PAIRS, 8, 128), jnp.float32),
            pltpu.VMEM((PLANES, PAIRS, 8, 128), jnp.float32),
            pltpu.VMEM((PLANES, PAIRS, 8, 128), jnp.float32),
            pltpu.VMEM((PLANES, PAIRS, 8, 128), jnp.float32),
            pltpu.VMEM((STEPS // 2 + 1, LATTICE, 2, ROWS, 128), jnp.float32),
            pltpu.VMEM((STEPS // 2, LATTICE, 2, ROWS, 128), jnp.float32),
            pltpu.VMEM((5, 2, ROWS, 128), jnp.float32),
            pltpu.VMEM((ROWS, 128), jnp.float32),
            pltpu.VMEM((STEPS, 3, 2, ROWS, 128), jnp.float32),
            pltpu.VMEM((5, 2, ROWS, 128), jnp.float32),
            pltpu.VMEM((16, 2 * LATTICE + 5, 8, 128), jnp.float32),
            pltpu.VMEM((128, 128), jnp.float32),
            pltpu.VMEM((128, 128), jnp.float32),
            pltpu.VMEM((16, 4, 128), jnp.float32),
            pltpu.VMEM((16, 4, 128), jnp.float32),
            pltpu.SemaphoreType.DMA((4,)),
            pltpu.SemaphoreType.DMA((12,)),
            pltpu.SemaphoreType.DMA((12,)),
            pltpu.SemaphoreType.DMA((16,)),
            pltpu.SemaphoreType.DMA((16,)),
        ],
        compiler_params=pltpu.CompilerParams(
            collective_id=0, has_side_effects=True, vmem_limit_bytes=50 * 1024 * 1024
        ),
    )(*[pltpu.with_memory_space_constraint(value, pltpu.HBM) for value in arguments])
    return (lattice[None], water)


def solution(mesh):
    in_specs = (
        P("side", None, None, "gx", "gy"),
        P("side", None, "gx", "gy"),
        P(None, "gx", ("side", "gy")),
        P("gx", ("side", "gy")),
    )
    out_specs = (P("side", None, None, "gx", "gy"), P(None, "gx", ("side", "gy")))
    return jax.shard_map(
        on_device, mesh=mesh, in_specs=in_specs, out_specs=out_specs, check_vma=False
    )
```

time: 71.4 us -> 38.7 us (0.54)
  Pallas kernels: 64.7 us -> 35.8 us
  local copies, waits for them, and re-layouts: 5.71 us -> 1.83 us
    pallas_call x1, Pallas kernels: 64.7 us -> 35.8 us  [on_device(): pl.pallas_call(step_kernel, out_shape=(jax.ShapeDtypeStruct(populations.s...]
    unnamed x10 -> x2, local copies, waits for them, and re-layouts: 5.71 us -> 1.83 us
where the time goes in v1:
time: 38.7 us; the launch traced here: 38.3 us
  Pallas kernels  35.8 us (93%)
  local copies, waits for them, and re-layouts  1.83 us (5%)
  between operations  0.64 us (2%)
    pallas_call x1, Pallas kernels, on_device(): pl.pallas_call(step_kernel, out_shape=(jax.ShapeDtypeStruct(populations.s...  35.8 us
    unnamed x2, local copies, waits for them, and re-layouts  1.83 us

profile of v1, /device:TPU:1, one launch (start us, length us, event | category | flops | bytes accessed | tf_op | source)
XLA Modules:
  0.0 38.3 jit_solution(9288818524744971285)
XLA Ops:
  0.6 35.8 %shard_map.59 = (f32[19,4,32,128]{3,2,1,0:T(8,128)S(1)}, f32[32,32,64]{2,1,0:T(8,128)S(1)}) custom-call(f32[19,4,32,128]{3,2,1,0:T(8,128)} %bitcast.4, s32[4,32,128]{2,1,0:T(8,128)} %bitcast.5, f32[32,32,64]{2,1,0:T(8,128)} %water_hbm.1, f32[32,64]{1,0:T(8,128)} %current_hbm.1), custom_call_target="tpu_custom_call" | custom-call | tf_op jit(solution)/shard_map/pallas_call | solution.py:543
  36.5 1.0 %copy.8 = f32[1,19,4,32,128]{4,3,2,1,0:T(8,128)} copy(f32[1,19,4,32,128]{4,3,2,1,0:T(8,128)S(1)} %bitcast.3) | data formatting | bytes 2490368
  37.5 0.8 %copy.9 = f32[32,32,64]{2,1,0:T(8,128)} copy(f32[32,32,64]{2,1,0:T(8,128)S(1)} %get-tuple-element.9) | data formatting | bytes 524288

commit v2 on v1

--- a/solution.py
+++ b/solution.py
@@ -125,7 +125,8 @@
     current_hbm,
     out_ref,
     sheet_ref,
-    raw,
+    window,
+    flux_window,
     raw_mask,
     water_ref,
     current_ref,
@@ -170,7 +171,7 @@
     loads = [
         pltpu.make_async_copy(source, target, load_sem.at[k])
         for k, (source, target) in enumerate(
-            ((pop_hbm, raw), (mask_hbm, raw_mask), (water_hbm, water_ref), (current_hbm, current_ref))
+            ((pop_hbm, window.at[pl.ds(0, LATTICE), :, :, pl.ds(16, 32), :]), (mask_hbm, raw_mask), (water_hbm, water_ref), (current_hbm, current_ref))
         )
     ]
     for load in loads:
@@ -178,7 +179,7 @@
 
     copies = []
 
-    def send(src, dst, device):
+    def prepare(src, dst, device):
         slot = len(copies)
         copy = pltpu.make_async_remote_copy(
             src_ref=src,
@@ -188,18 +189,36 @@
             device_id=device,
             device_id_type=MESH,
         )
-        copy.start()
         copies.append(copy)
         return copy
 
+    def send(src, dst, device):
+        copy = prepare(src, dst, device)
+        copy.start()
+        return copy
+
     loads[0].wait()
-    for i in range(LATTICE):
-        turned = jnp.swapaxes(raw[i].reshape(128, 128), 0, 1)
-        own[i, 1:9] = turned.reshape(8, 2, 8, 128)
+    pl.semaphore_wait(barrier, groups + 1)
+
+    lattice = pl.ds(0, LATTICE)
+    edges = ((16, 48, x_down), (32, 0, x_up))
+    x_copies = [
+        send(
+            window.at[lattice, :, :, pl.ds(source, 16), :], window.at[lattice, :, :, pl.ds(target, 16), :], device
+        )
+        for source, target, device in edges
+    ]
     loads[1].wait()
-    own[MASK_PLANE, 1:9] = jnp.swapaxes(
-        raw_mask[...].astype(jnp.float32).reshape(128, 128), 0, 1
-    ).reshape(8, 2, 8, 128)
+    window[MASK_PLANE, :, :, 16:48, :] = raw_mask[...].astype(jnp.float32)
+    x_copies += [
+        send(
+            window.at[MASK_PLANE, :, :, pl.ds(source, 16), :],
+            window.at[MASK_PLANE, :, :, pl.ds(target, 16), :],
+            device,
+        )
+        for source, target, device in edges
+    ]
+
     loads[2].wait()
     loads[3].wait()
     square[0:32, 0:64] = water_ref[0]
@@ -211,27 +230,13 @@
             send_pieces[s * 8 + g, 2:4, :] = faces[2 * g : 2 * g + 2]
     total = None
     for i in range(LATTICE):
-        part = own[i, 1:9].reshape(128, 128)
+        part = window[i, 0, 0, 16:48, :]
         total = part if total is None else total + part
-    columns[...] = total
+    square[0:32, :] = total
+    columns[...] = jnp.swapaxes(square[...], 0, 1)
     surface = pack_columns(columns, 0, 32)
     for c in range(16):
         send_pieces[c, 0:2, :] = surface[2 * c : 2 * c + 2]
-    main = pl.ds(0, LATTICE + 1)
-    inner = pl.ds(1, 8)
-
-    def pack_planes(i):
-        low, high = pack_pair(own[i, 1:9, 0], own[i, 1:9, 1])
-        pack_low[i, 1:9] = low
-        pack_high[i, 1:9] = high
-
-    def pack_four(k, carry):
-        for i in range(4):
-            pack_planes(4 * k + i)
-        return carry
-
-    lax.fori_loop(0, (LATTICE + 1) // 4, pack_four, 0)
-    pl.semaphore_wait(barrier, groups + 1)
     pieces = []
     for d in range(1, groups):
         other, device = peer(d)
@@ -246,13 +251,14 @@
         copy.start()
         pieces.append(copy)
 
+    for i in range(LATTICE + 1):
+        turned = jnp.swapaxes(window[i, :, :, 16:48, :].reshape(128, 128), 0, 1)
+        own[i, 1] = turned[0:16].reshape(2, 8, 128)
+        own[i, 8] = turned[112:128].reshape(2, 8, 128)
+    main = pl.ds(0, LATTICE + 1)
     y_copies = [
         send(own.at[main, 8], own.at[main, 0], y_up),
         send(own.at[main, 1], own.at[main, 9], y_down),
-    ]
-    x_copies = [
-        send(pack_low.at[main, inner], halo_high.at[main, inner], x_down),
-        send(pack_high.at[main, inner], halo_low.at[main, inner], x_up),
     ]
 
     lane = lanes_of((8, 128))
@@ -274,6 +280,13 @@
                 else:
                     yield i, k, [flux.at[rows, :], None]
 
+    def set_coefficients(g, rows, pore):
+        coefficients[0, g, rows, :] = pore
+        coefficients[1, g, rows, :] = (3.0 * KAPPA) * pore
+        coefficients[2, g, rows, :] = (0.5 + 0.5 * (RATE - 1.0)) * pore - 0.5
+        coefficients[3, g, rows, :] = 0.5 - (0.5 - 0.5 * (RATE - 1.0)) * pore
+        coefficients[4, g, rows, :] = 1.0 - RATE * pore
+
     def place_own(t, planes):
         for i, k, targets in planes_at(t, planes):
             tile = own[i, t, k]
@@ -281,9 +294,9 @@
                 if target is not None:
                     target[...] = roll(tile, shift)
 
-    def place_halo(t):
-        for i, k, targets in planes_at(t, range(PLANES)):
-            low, high = halo_low[i, t], halo_high[i, t]
+    def place_halo(t, planes):
+        for i, k, targets in planes_at(t, planes):
+            low, high = halo_low[i, t // 9], halo_high[i, t // 9]
             for g, target in enumerate(targets):
                 if target is not None:
                     pltpu.store(target, roll(low, -16 * k - 32 * g), mask=is_low)
@@ -292,17 +305,7 @@
         for k in range(2):
             rows = pl.ds(start + 8 * k, 8)
             for g in range(2):
-                pore = coefficients[0, g, rows, :]
-                coefficients[1, g, rows, :] = (3.0 * KAPPA) * pore
-                coefficients[2, g, rows, :] = (0.5 + 0.5 * (RATE - 1.0)) * pore - 0.5
-                coefficients[3, g, rows, :] = 0.5 - (0.5 - 0.5 * (RATE - 1.0)) * pore
-                coefficients[4, g, rows, :] = 1.0 - RATE * pore
-
-    def place_inner(t, carry):
-        place_own(t, range(LATTICE + 1))
-        return carry
-
-    lax.fori_loop(1, 9, place_inner, 0)
+                set_coefficients(g, rows, coefficients[0, g, rows, :])
 
     recv_pieces[me] = send_pieces[me]
     for copy in pieces:
@@ -313,43 +316,44 @@
     own_surface = columns[...]
     unpack_columns(square[0:32, :], columns)
     own_inflow = uptake_rate * (uptake(own_surface) - columns[...])
-    own[FLUX_PLANE, 1:9] = own_inflow.reshape(8, 2, 8, 128)
+    own[FLUX_PLANE, 1] = own_inflow[0:16].reshape(2, 8, 128)
+    own[FLUX_PLANE, 8] = own_inflow[112:128].reshape(2, 8, 128)
+    flux_window[16:48, :] = jnp.swapaxes(own_inflow, 0, 1)[0:32]
     y_copies += [
         send(own.at[FLUX_PLANE, 8], own.at[FLUX_PLANE, 0], y_up),
         send(own.at[FLUX_PLANE, 1], own.at[FLUX_PLANE, 9], y_down),
     ]
-    pack_planes(FLUX_PLANE)
     x_copies += [
-        send(pack_low.at[FLUX_PLANE, inner], halo_high.at[FLUX_PLANE, inner], x_down),
-        send(pack_high.at[FLUX_PLANE, inner], halo_low.at[FLUX_PLANE, inner], x_up),
+        send(flux_window.at[pl.ds(source, 16), :], flux_window.at[pl.ds(target, 16), :], device)
+        for source, target, device in edges
     ]
     unpack_columns(square[32:64, :], columns)
     square[...] = jnp.swapaxes(columns[...], 0, 1)
     sheet_update(water_ref, current_ref, square, sheet_ref)
 
-    for t in range(1, 9):
-        place_own(t, [FLUX_PLANE])
-    for copy in y_copies:
-        copy.wait()
+    corner_copies = []
+    for end in range(2):
+        corner_copies += [
+            prepare(pack_low.at[:, end], halo_high.at[:, end], x_down),
+            prepare(pack_high.at[:, end], halo_low.at[:, end], x_up),
+        ]
 
     def pack_corners(k, carry):
         for i in range(3):
             for t in (0, 9):
                 low, high = pack_pair(own[3 * k + i, t, 0], own[3 * k + i, t, 1])
-                pack_low[3 * k + i, t] = low
-                pack_high[3 * k + i, t] = high
+                pack_low[3 * k + i, t // 9] = low
+                pack_high[3 * k + i, t // 9] = high
         return carry
 
-    lax.fori_loop(0, PLANES // 3, pack_corners, 0)
-    corner_copies = []
-    for t in (0, 9):
-        corner_copies += [
-            send(pack_low.at[:, t], halo_high.at[:, t], x_down),
-            send(pack_high.at[:, t], halo_low.at[:, t], x_up),
-        ]
-
-    for t in (0, 9):
-        place_own(t, range(PLANES))
+    def pass_corners():
+        for copy in y_copies:
+            copy.wait()
+        lax.fori_loop(0, PLANES // 3, pack_corners, 0)
+        for copy in corner_copies:
+            copy.start()
+        for t in (0, 9):
+            place_own(t, range(PLANES))
 
     zero = jnp.zeros((8, 128), jnp.float32)
 
@@ -511,33 +515,43 @@
 
         lax.fori_loop(begin // 2, end // 2, two_steps, 0)
 
-    for copy in x_copies:
+    for copy in x_copies[:4]:
         copy.wait()
-
-    def halo_inner(t, carry):
-        place_halo(t)
-        return carry
-
-    lax.fori_loop(1, 9, halo_inner, 0)
+    for i in range(LATTICE + 1):
+        for g in range(2):
+            turned = jnp.swapaxes(window[i, :, g].reshape(128, 128), 0, 1)
+            if i < LATTICE:
+                fields_even[0, i, g, pl.ds(PAD + 16 - velocity_table[i][1], 128), :] = turned
+            else:
+                set_coefficients(g, pl.ds(PAD + 16, 128), turned)
+    for copy in x_copies[4:]:
+        copy.wait()
+    flux[pl.ds(PAD + 16, 128), :] = jnp.swapaxes(flux_window[...], 0, 1)
+    pass_corners()
     run_steps(range(2, 18), 0, STEPS)
     for copy in corner_copies:
         copy.wait()
     for t in (0, 9):
-        place_halo(t)
+        place_halo(t, range(PLANES))
     for base in range(2):
         ends = [base + k for k in range(3)] + [17 - base + k for k in range(3)]
         run_steps(ends, base * STEPS // 2, (base + 1) * STEPS // 2)
 
-    even_layer = lanes_of((128, 128)) // 32 % 2 == 0
     for i in range(LATTICE):
         rows = pl.ds(PAD + 16 - velocity_table[i][1], 128)
-        a, b = fields_even[STEPS // 2, i, 0, rows, :], fields_even[STEPS // 2, i, 1, rows, :]
-        merged = jnp.where(even_layer, roll(a, -16), roll(b, 16))
-        out_ref[i] = jnp.swapaxes(merged, 0, 1).reshape(4, 32, 128)
+        for g in range(2):
+            turned = jnp.swapaxes(fields_even[STEPS // 2, i, g, rows, :], 0, 1)
+            out_ref[i, g] = turned[16:48]
+            out_ref[i, g + 2] = turned[80:112]
 
 
 def on_device(populations, solid_mask, water_sheet, current):
-    arguments = (populations[0], solid_mask[0], water_sheet, current)
+    arguments = (
+        populations.reshape(LATTICE, 2, 2, 32, 128),
+        solid_mask.reshape(2, 2, 32, 128),
+        water_sheet,
+        current,
+    )
     vmem = pl.BlockSpec(memory_space=pltpu.VMEM)
     hbm = pl.BlockSpec(memory_space=pltpu.HBM)
     lattice, water = pl.pallas_call(
@@ -549,15 +563,16 @@
         in_specs=[hbm, hbm, hbm, hbm],
         out_specs=(vmem, vmem),
         scratch_shapes=[
-            pltpu.VMEM((LATTICE, 4, 32, 128), jnp.float32),
-            pltpu.VMEM(solid_mask.shape[1:], jnp.int32),
+            pltpu.VMEM((LATTICE + 1, 2, 2, 64, 128), jnp.float32),
+            pltpu.VMEM((128, 128), jnp.float32),
+            pltpu.VMEM((2, 2, 32, 128), jnp.int32),
             pltpu.VMEM(water_sheet.shape, jnp.float32),
             pltpu.VMEM(current.shape, jnp.float32),
             pltpu.VMEM((PLANES, PAIRS, 2, 8, 128), jnp.float32),
-            pltpu.VMEM((PLANES, PAIRS, 8, 128), jnp.float32),
-            pltpu.VMEM((PLANES, PAIRS, 8, 128), jnp.float32),
-            pltpu.VMEM((PLANES, PAIRS, 8, 128), jnp.float32),
-            pltpu.VMEM((PLANES, PAIRS, 8, 128), jnp.float32),
+            pltpu.VMEM((PLANES, 2, 8, 128), jnp.float32),
+            pltpu.VMEM((PLANES, 2, 8, 128), jnp.float32),
+            pltpu.VMEM((PLANES, 2, 8, 128), jnp.float32),
+            pltpu.VMEM((PLANES, 2, 8, 128), jnp.float32),
             pltpu.VMEM((STEPS // 2 + 1, LATTICE, 2, ROWS, 128), jnp.float32),
             pltpu.VMEM((STEPS // 2, LATTICE, 2, ROWS, 128), jnp.float32),
             pltpu.VMEM((5, 2, ROWS, 128), jnp.float32),
@@ -570,8 +585,8 @@
             pltpu.VMEM((16, 4, 128), jnp.float32),
             pltpu.VMEM((16, 4, 128), jnp.float32),
             pltpu.SemaphoreType.DMA((4,)),
-            pltpu.SemaphoreType.DMA((12,)),
-            pltpu.SemaphoreType.DMA((12,)),
+            pltpu.SemaphoreType.DMA((16,)),
+            pltpu.SemaphoreType.DMA((16,)),
             pltpu.SemaphoreType.DMA((16,)),
             pltpu.SemaphoreType.DMA((16,)),
         ],

time: 38.7 us -> 37.5 us (0.969)
  Pallas kernels: 35.8 us -> 34.9 us
    pallas_call x1, Pallas kernels: 35.8 us -> 34.9 us  [on_device(): pl.pallas_call(step_kernel, out_shape=(jax.ShapeDtypeStruct(populations.s...]
where the time goes in v2:
time: 37.5 us; the launch traced here: 37.3 us
  Pallas kernels  34.9 us (93%)
  local copies, waits for them, and re-layouts  1.83 us (5%)
  between operations  0.64 us (2%)
    pallas_call x1, Pallas kernels, on_device(): pl.pallas_call(step_kernel, out_shape=(jax.ShapeDtypeStruct(populations.s...  34.9 us
    unnamed x2, local copies, waits for them, and re-layouts  1.83 us

profile of v2, /device:TPU:1, one launch (start us, length us, event | category | flops | bytes accessed | tf_op | source)
XLA Modules:
  0.0 37.3 jit_solution(6240440549657857232)
XLA Ops:
  0.6 34.9 %shard_map.59 = (f32[19,4,32,128]{3,2,1,0:T(8,128)S(1)}, f32[32,32,64]{2,1,0:T(8,128)S(1)}) custom-call(f32[19,2,2,32,128]{4,3,2,1,0:T(8,128)} %bitcast.4, s32[2,2,32,128]{3,2,1,0:T(8,128)} %bitcast.5, f32[32,32,64]{2,1,0:T(8,128)} %water_hbm.1, f32[32,64]{1,0:T(8,128)} %current_hbm.1), custom_call_target="tpu_custom_call" | custom-call | tf_op jit(solution)/shard_map/pallas_call | solution.py:557
  35.5 1.0 %copy.8 = f32[1,19,4,32,128]{4,3,2,1,0:T(8,128)} copy(f32[1,19,4,32,128]{4,3,2,1,0:T(8,128)S(1)} %bitcast.3) | data formatting | bytes 2490368
  36.5 0.8 %copy.9 = f32[32,32,64]{2,1,0:T(8,128)} copy(f32[32,32,64]{2,1,0:T(8,128)S(1)} %get-tuple-element.9) | data formatting | bytes 524288

commit v3 on v2

--- a/solution.py
+++ b/solution.py
@@ -494,7 +494,7 @@
                 wall = stage[half, LATTICE + opposite_index[i]]
                 pltpu.store(fields.at[i, 1, moved, :], wall, mask=last)
 
-    def run_steps(tiles, begin, end):
+    def run_steps(tiles, begin, end, after_two=None):
         starts = [tile * 8 + PAD for tile in tiles]
 
         def one_step(step, now, then):
@@ -511,6 +511,8 @@
         def two_steps(half, carry):
             one_step(2 * half, fields_even.at[half], fields_odd.at[half])
             one_step(2 * half + 1, fields_odd.at[half], fields_even.at[half + 1])
+            if after_two is not None:
+                pl.when(half == begin // 2)(after_two)
             return carry
 
         lax.fori_loop(begin // 2, end // 2, two_steps, 0)
@@ -527,8 +529,7 @@
     for copy in x_copies[4:]:
         copy.wait()
     flux[pl.ds(PAD + 16, 128), :] = jnp.swapaxes(flux_window[...], 0, 1)
-    pass_corners()
-    run_steps(range(2, 18), 0, STEPS)
+    run_steps(range(2, 18), 0, STEPS, pass_corners)
     for copy in corner_copies:
         copy.wait()
     for t in (0, 9):

time: 37.5 us -> 37.5 us (level)
  no operation moved by 1% of the time
where the time goes in v3:
time: 37.5 us; the launch traced here: 37.3 us
  Pallas kernels  34.9 us (93%)
  local copies, waits for them, and re-layouts  1.83 us (5%)
  between operations  0.64 us (2%)
    pallas_call x1, Pallas kernels, on_device(): pl.pallas_call(step_kernel, out_shape=(jax.ShapeDtypeStruct(populations.s...  34.9 us
    unnamed x2, local copies, waits for them, and re-layouts  1.83 us

profile of v3, /device:TPU:1, one launch (start us, length us, event | category | flops | bytes accessed | tf_op | source)
XLA Modules:
  0.0 37.3 jit_solution(8288012051933079520)
XLA Ops:
  0.6 34.9 %shard_map.59 = (f32[19,4,32,128]{3,2,1,0:T(8,128)S(1)}, f32[32,32,64]{2,1,0:T(8,128)S(1)}) custom-call(f32[19,2,2,32,128]{4,3,2,1,0:T(8,128)} %bitcast.4, s32[2,2,32,128]{3,2,1,0:T(8,128)} %bitcast.5, f32[32,32,64]{2,1,0:T(8,128)} %water_hbm.1, f32[32,64]{1,0:T(8,128)} %current_hbm.1), custom_call_target="tpu_custom_call" | custom-call | tf_op jit(solution)/shard_map/pallas_call | solution.py:558
  35.5 1.0 %copy.8 = f32[1,19,4,32,128]{4,3,2,1,0:T(8,128)} copy(f32[1,19,4,32,128]{4,3,2,1,0:T(8,128)S(1)} %bitcast.3) | data formatting | bytes 2490368
  36.5 0.8 %copy.9 = f32[32,32,64]{2,1,0:T(8,128)} copy(f32[32,32,64]{2,1,0:T(8,128)S(1)} %get-tuple-element.9) | data formatting | bytes 524288
